TPU v7x, 32 devices: a whole 2x2x4 slice. The times are simulated.
32 devices in a mesh: row: 16 (over z, x, core), col: 2 (over y).
Axes of the slice: x: 2, y: 2, z: 4, core: 2. Of those that a mesh axis runs over, the one named last changes fastest.
Arguments:
- embed_first: bfloat16 [768, 16384], P('col', 'row'), may hold values from -6 to 6
- embed_second: bfloat16 [768, 16384], P('row', 'col'), may hold values from -6 to 6
- corr_grad: float32 [16384, 16384], P('row', 'col'), may hold values from -0.046875 to 0.046875
Outputs:
- grad_first: bfloat16 [768, 16384], P('col', 'row')
- grad_second: bfloat16 [768, 16384], P('row', 'col')
All inputs are finite; a program needn't handle non-finite values.
Results may differ from a plain program's by a relative error of at most 0.0065.
Values may be sent and summed in bfloat16 or wider, within the bound.
A program may use at most 128 MiB of HBM per device.

v0:
```python
import jax
import jax.numpy as jnp
from jax import lax
from jax.sharding import PartitionSpec as P


def local(embed_first, embed_second, corr_grad):
    low_grad = corr_grad.astype(jnp.bfloat16)
    first_terms = lax.dot_general(
        lax.all_gather(embed_second, "row", axis=0, tiled=True),
        low_grad,
        (((1,), (1,)), ((), ())),
        preferred_element_type=jnp.float32,
    )
    grad_first = lax.psum_scatter(first_terms, "col", scatter_dimension=0, tiled=True).astype(
        jnp.bfloat16
    )
    whole_first = lax.all_gather(embed_first, "col", axis=0, tiled=True)
    grad_second = lax.psum_scatter(
        jnp.dot(whole_first, low_grad, preferred_element_type=jnp.float32),
        "row",
        scatter_dimension=0,
        tiled=True,
    ).astype(jnp.bfloat16)
    return (grad_first, grad_second)


def solution(mesh):
    return jax.shard_map(
        local,
        mesh=mesh,
        in_specs=(P("col", "row"), P("row", "col"), P("row", "col")),
        out_specs=(P("col", "row"), P("row", "col")),
        check_vma=False,
    )
```

profile of v0, /device:TPU:0, one launch (start us, length us, event | category | flops | bytes accessed | tf_op | source)
XLA Modules:
  0.0 442.6 jit_solution(5744932077926208321)
XLA Ops:
  7.2 0.0 all-gather.3.cloned.1.call-start
  7.2 0.7 all-gather.3.cloned.1.call-update
  7.9 0.0 all-gather.5.cloned.1.call-start
  7.9 0.7 all-gather.5.cloned.1.call-update
  8.6 0.0 reduce-scatter.3.cloned.1.call-start
  8.7 104.7 %all-gather.3.cloned.1.call-done = bf16[768,8192]{1,0:T(8,128)(2,1)} async-done(((bf16[48,8192]{1,0:T(8,128)(2,1)}), bf16[768,8192]{1,0:T(8,128)(2,1)}) %all-gather.3.cloned.1.call-update) | async-done | bytes 12582928 | tf_op jit(solution)/shard_map/all_gather | solution.py:10
  113.4 22.0 %fusion.2 = f32[768,1024]{1,0:T(8,128)} fusion(bf16[768,8192]{1,0:T(8,128)(2,1)} %all-gather.3.cloned.1.call-done, f32[1024,8192]{1,0:T(8,128)} %param.5), kind=kOutput, calls=%fused_computation.2 | convolution fusion | flops 12893290496 | bytes 49283072 | tf_op jit(solution)/shard_map/dot_general | solution.py:9
  135.4 0.0 reduce-scatter.3.cloned.1.call-update
  135.4 0.0 reduce-scatter.5.cloned.1.call-start
  135.5 5.0 %all-gather.5.cloned.1.call-done = bf16[768,1024]{1,0:T(8,128)(2,1)} async-done(((bf16[384,1024]{1,0:T(8,128)(2,1)}), bf16[768,1024]{1,0:T(8,128)(2,1)}) %all-gather.5.cloned.1.call-update) | async-done | bytes 1572880 | tf_op jit(solution)/shard_map/all_gather | solution.py:18
  140.4 27.3 %fusion = f32[768,8192]{1,0:T(8,128)} fusion(bf16[768,1024]{1,0:T(8,128)(2,1)} %all-gather.5.cloned.1.call-done, f32[1024,8192]{1,0:T(8,128)} %param.5), kind=kOutput, calls=%fused_computation | convolution fusion | flops 12893290496 | bytes 60293120 | tf_op jit(solution)/shard_map/dot_general | solution.py:20
  167.7 0.0 reduce-scatter.5.cloned.1.call-update
  167.7 18.4 %reduce-scatter.3.cloned.1.call-done = f32[384,1024]{1,0:T(8,128)} async-done(((f32[768,1024]{1,0:T(8,128)}), f32[384,1024]{1,0:T(8,128)}) %reduce-scatter.3.cloned.1.call-update) | async-done | bytes 1572880 | tf_op jit(solution)/shard_map/reduce_scatter | solution.py:15
  186.2 2.4 convert_element_type.10
  188.6 245.1 %reduce-scatter.5.cloned.1.call-done = f32[48,8192]{1,0:T(8,128)} async-done(((f32[768,8192]{1,0:T(8,128)}), f32[48,8192]{1,0:T(8,128)}) %reduce-scatter.5.cloned.1.call-update) | async-done | bytes 1572880 | tf_op jit(solution)/shard_map/reduce_scatter | solution.py:19
  433.7 2.4 convert_element_type.11
Async XLA Ops:
  7.2 106.3 %all-gather.3.cloned.1.call-start = ((), (), s32[]{:S(2)}) async-start(), calls=%async_computation.2 | async-start | bytes 13369344 | tf_op jit(solution)/shard_map/all_gather | solution.py:10
  7.9 132.5 %all-gather.5.cloned.1.call-start = ((), (), s32[]{:S(2)}) async-start(), calls=%async_computation.4 | async-start | bytes 2359296 | tf_op jit(solution)/shard_map/all_gather | solution.py:18
  8.6 177.5 %reduce-scatter.3.cloned.1.call-start = ((), (), s32[]{:S(2)}) async-start(), calls=%async_computation.3 | async-start | bytes 4718592 | tf_op jit(solution)/shard_map/reduce_scatter | solution.py:15
  135.4 298.3 %reduce-scatter.5.cloned.1.call-start = ((), (), s32[]{:S(2)}) async-start(), calls=%async_computation.5 | async-start | bytes 26738688 | tf_op jit(solution)/shard_map/reduce_scatter | solution.py:19
Sparse Core Ops, SparseCore 0:
  10.3 103.1 all-gather.2
  115.0 25.4 all-gather.4
  142.7 43.4 reduce-scatter.2
  190.1 243.5 reduce-scatter.4
where the time goes:
time: 443 us
  waiting for transfers between devices  375 us (85%)
  matrix products  49.2 us (11%)
  between operations  13.8 us (3%)
  other arithmetic  4.77 us (1%)
    reduce_scatter x1, waiting for transfers between devices, local(): lax.psum_scatter(jnp.dot(whole_first, low_grad, preferred_element_type=jn...  245 us
    all_gather x1, waiting for transfers between devices, local(): lax.all_gather(embed_second, 'row', axis=0, tiled=True)  105 us
    dot_general x1, matrix products, local(): jnp.dot(whole_first, low_grad, preferred_element_type=jnp.float32)  27.3 us
    dot_general x1, matrix products, local(): lax.dot_general(lax.all_gather(embed_second, 'row', axis=0, tiled=True),...  22 us
    reduce_scatter x1, waiting for transfers between devices, local(): lax.psum_scatter(first_terms, 'col', scatter_dimension=0, tiled=True)  18.4 us
  transfers between devices with their start and end apart: 4, of which 4 were waited for; matrix products, arithmetic and copies ran while one was open for 12% of the time, Pallas kernels for 0%

commit v1 on v0

v1 whole, which is shorter than its diff:
```python
import functools

import jax
import jax.numpy as jnp
from jax import lax
from jax.experimental import pallas as pl
from jax.experimental.pallas import tpu as pltpu
from jax.sharding import PartitionSpec as P

PIECES = 4
TILE = 256
SLOTS = 3
EARLY = 3


def kernel(
    a_side, b_side, cols, early,
    e1_ref, e2_ref, g_ref, o1_ref, o2_ref,
    e1x, e2x, gb, p2, s2, rb, t1s, t1r, gt,
    g_sem, e1_send, e1_recv, ag_send, ag_recv, sib_send, sib_recv,
    d2d_send, d2d_recv, rs_send, rs_recv, t1_send, t1_recv,
):
    chips = a_side * b_side
    block, fj = e2_ref.shape
    rows, fi = e1_ref.shape
    share = chips // cols
    width = fj // PIECES
    half = PIECES // 2
    bf16, f32 = jnp.bfloat16, jnp.float32

    me = lax.axis_index("row")
    my_col = lax.axis_index("col")
    chip, core = me // 2, me % 2
    other = 1 - core

    def chip_at(pos):
        first = 1 - jnp.minimum(pos // a_side, 1)
        q = jnp.maximum(pos - a_side, 0)
        i, j = q // (b_side - 1), q % (b_side - 1)
        odd = i % 2
        b = (1 - odd) * (1 + j) + odd * (b_side - 1 - j)
        return first * (pos * b_side) + (1 - first) * ((a_side - 1 - i) * b_side + b)

    a, b = chip // b_side, chip % b_side
    i = a_side - 1 - a
    later = a_side + i * (b_side - 1) + (1 - i % 2) * (b - 1) + (i % 2) * (b_side - 1 - b)
    inner = jnp.minimum(b, 1)
    pos = (1 - inner) * a + inner * later

    def chip_off(offset):
        return chip_at((pos + offset + 2 * chips) % chips)

    right = chip_off(1) * 2 + core
    left = chip_off(-1) * 2 + core
    sibling = chip * 2 + other

    def piece(k):
        return pl.ds(k * width, width)

    def ahead(k):
        return right if k < half else left

    def sign(k):
        return 1 if k < half else -1

    def remote(src, dst, send, recv, **to):
        return pltpu.make_async_remote_copy(
            src_ref=src, dst_ref=dst, send_sem=send, recv_sem=recv,
            device_id=to, device_id_type=pl.DeviceIdType.MESH,
        )

    barrier = pltpu.get_barrier_semaphore()
    for to in (right, left, sibling):
        pl.semaphore_signal(barrier, inc=1, device_id={"row": to}, device_id_type=pl.DeviceIdType.MESH)
    for off in range(1, cols):
        pl.semaphore_signal(
            barrier, inc=1, device_id={"col": (my_col + off) % cols}, device_id_type=pl.DeviceIdType.MESH
        )
    pl.semaphore_wait(barrier, 3 + cols - 1)

    def gather_copy(t, k, first=False):
        src_chip = chip_off(-sign(k) * t)
        dst = e2x.at[src_chip, core, :, piece(k)]
        src = e2_ref.at[:, piece(k)] if first else dst
        return remote(src, dst, ag_send.at[t, k], ag_recv.at[t, k], row=ahead(k))

    def sibling_copy(t, k, first=False):
        src_chip = chip_off(-sign(k) * t)
        dst = e2x.at[src_chip, core, :, piece(k)]
        src = e2_ref.at[:, piece(k)] if first else dst
        return remote(src, dst, sib_send.at[t, k], sib_recv.at[t, k], row=sibling)

    def gather_step(t, last=False):
        for k in range(PIECES):
            gather_copy(t, k).wait_recv()
            if not last:
                gather_copy(t + 1, k).start()
            sibling_copy(t + 1, k).start()

    order = [k for pair in zip(range(half), range(half, PIECES)) for k in pair]
    for k in order:
        gather_copy(0, k, True).start()
    e1_copies = []
    for off in range(1, cols):
        to = (my_col + off) % cols
        e1_copies.append(remote(e1_ref, e1x.at[off - 1], e1_send.at[off - 1], e1_recv.at[off - 1], col=to))
        e1_copies[-1].start()

    def load(n):
        slot = n % SLOTS
        return pltpu.make_async_copy(
            g_ref.at[:, pl.ds(pl.multiple_of(n * TILE, TILE), TILE)], gt.at[slot], g_sem.at[slot]
        )

    tiles = fj // TILE
    for n in range(SLOTS):
        load(n).start()
    for k in order:
        sibling_copy(0, k, True).start()

    def first_pass(n, carry):
        load(n).wait()
        at = pl.ds(pl.multiple_of(n * TILE, TILE), TILE)
        low = gt[n % SLOTS].astype(bf16)
        gb[:, at] = low

        @pl.when(n + SLOTS < tiles)
        def _():
            load(n + SLOTS).start()

        terms = jnp.dot(e1_ref[...], low, preferred_element_type=f32).astype(bf16)
        p2[pl.ds(my_col * share, share), :, :, at] = terms.reshape(share, 2, block, TILE)
        return carry

    def next_pass(off, wide):
        from_col = (my_col - off + cols) % cols

        def body(n, carry):
            at = pl.ds(pl.multiple_of(n * wide, wide), wide)
            terms = jnp.dot(e1x[off - 1], gb[:, at], preferred_element_type=f32).astype(bf16)
            p2[pl.ds(from_col * share, share), :, :, at] = terms.reshape(share, 2, block, wide)
            return carry

        return body

    def d2d_copy(off, h):
        from_chip = pl.ds((my_col - off + cols) % cols * share, share)
        at = pl.ds(h * (fj // 2), fj // 2)
        return remote(
            p2.at[from_chip, other, :, at], s2.at[from_chip, :, at],
            d2d_send.at[off, h], d2d_recv.at[off, h], row=sibling,
        )

    taken = 0
    for h in range(2):
        lax.fori_loop(h * tiles // 2, (h + 1) * tiles // 2, first_pass, 0)
        d2d_copy(0, h).start()
    gather_step(taken)
    taken += 1
    e2x[chip, core] = e2_ref[...]
    wide = 512
    for off in range(1, cols):
        e1_copies[off - 1].wait_recv()
        for h in range(2):
            lax.fori_loop(h * fj // wide // 2, (h + 1) * fj // wide // 2, next_pass(off, wide), 0)
            d2d_copy(off, h).start()
        if taken < early:
            gather_step(taken)
            taken += 1
    while taken < early:
        gather_step(taken)
        taken += 1
    for off in range(cols):
        for h in range(2):
            d2d_copy(off, h).wait_recv()

    def sum_copy(t, k):
        to_chip = chip_off(-sign(k) * (t + 1))
        return remote(
            p2.at[to_chip, core, :, piece(k)], rb.at[t, :, piece(k)],
            rs_send.at[t, k], rs_recv.at[t, k], row=ahead(k),
        )

    def sum_first():
        for k in order:
            to_chip = chip_off(-sign(k))
            at = piece(k)
            total = p2[to_chip, core, :, at].astype(f32) + s2[to_chip, :, at].astype(f32)
            p2[to_chip, core, :, at] = total.astype(bf16)
            sum_copy(0, k).start()

    def sum_step(t):
        for k in order:
            to_chip = chip_off(-sign(k) * (t + 1))
            at = piece(k)
            sum_copy(t - 1, k).wait_recv()
            total = p2[to_chip, core, :, at].astype(f32) + s2[to_chip, :, at].astype(f32)
            total += rb[t - 1, :, at].astype(f32)
            p2[to_chip, core, :, at] = total.astype(bf16)
            sum_copy(t, k).start()

    sum_first()
    steps = chips - 1

    def both(t, carry):
        gather_step(t + early - 1)
        sum_step(t)
        return carry

    lax.fori_loop(1, steps - early, both, 0)
    done = steps - early
    gather_step(steps - 1, last=True)
    sum_step(done)
    done += 1
    for t in range(chips):
        for k in range(PIECES):
            sibling_copy(t, k).wait_recv()

    def t1_copy(off):
        return remote(
            t1s.at[off - 1], t1r.at[off - 1], t1_send.at[off - 1], t1_recv.at[off - 1],
            col=(my_col + off) % cols,
        )

    def first_terms(of_col, n):
        left_side = e2x[pl.ds(of_col * share, share)].reshape(rows, fj)
        part = gb[pl.ds(pl.multiple_of(n * TILE, TILE), TILE), :]
        return lax.dot_general(left_side, part, (((1,), (1,)), ((), ())), preferred_element_type=f32)

    for off in range(1, cols):
        def send_body(n, carry, off=off):
            at = pl.ds(pl.multiple_of(n * TILE, TILE), TILE)
            t1s[off - 1, :, at] = first_terms((my_col + off) % cols, n).astype(bf16)
            return carry

        lax.fori_loop(0, fi // TILE, send_body, 0)
        t1_copy(off).start()
        if done < steps:
            sum_step(done)
            done += 1

    def keep(n):
        return gt.at[n // 2, pl.ds(pl.multiple_of(n % 2 * rows, rows), rows)]

    def own_body(n, carry):
        keep(n)[...] = first_terms(my_col, n)
        return carry

    lax.fori_loop(0, fi // TILE, own_body, 0)
    while done < steps:
        sum_step(done)
        done += 1

    for off in range(1, cols):
        t1_copy(off).wait_recv()

    def out_body(n, carry):
        at = pl.ds(pl.multiple_of(n * TILE, TILE), TILE)
        total = keep(n)[...]
        for off in range(1, cols):
            total += t1r[off - 1, :, at].astype(f32)
        o1_ref[:, at] = total.astype(bf16)
        return carry

    lax.fori_loop(0, fi // TILE, out_body, 0)

    for k in order:
        at = piece(k)
        sum_copy(steps - 1, k).wait_recv()
        total = p2[chip, core, :, at].astype(f32) + s2[chip, :, at].astype(f32)
        o2_ref[:, at] = (total + rb[steps - 1, :, at].astype(f32)).astype(bf16)

    for t in range(steps):
        for k in range(PIECES):
            gather_copy(t, k).wait_send()
            sum_copy(t, k).wait_send()
    for t in range(chips):
        for k in range(PIECES):
            sibling_copy(t, k).wait_send()
    for off in range(cols):
        for h in range(2):
            d2d_copy(off, h).wait_send()
    for off in range(1, cols):
        e1_copies[off - 1].wait_send()
        t1_copy(off).wait_send()


def local(rows_size, cols, e1, e2, g):
    chips = rows_size // 2
    a_side = 4
    b_side = chips // a_side
    block, fj = e2.shape
    rows, fi = e1.shape
    bf16 = jnp.bfloat16
    vmem = pl.BlockSpec(memory_space=pltpu.VMEM)
    dma = pltpu.SemaphoreType.DMA
    steps = chips - 1
    return pl.pallas_call(
        functools.partial(kernel, a_side, b_side, cols, min(EARLY, steps - 2)),
        out_shape=(jax.ShapeDtypeStruct(e1.shape, bf16), jax.ShapeDtypeStruct(e2.shape, bf16)),
        in_specs=[vmem, vmem, pl.BlockSpec(memory_space=pl.ANY)],
        out_specs=(vmem, vmem),
        scratch_shapes=[
            pltpu.VMEM((cols - 1, rows, fi), bf16),
            pltpu.VMEM((chips, 2, block, fj), bf16),
            pltpu.VMEM((fi, fj), bf16),
            pltpu.VMEM((chips, 2, block, fj), bf16),
            pltpu.VMEM((chips, block, fj), bf16),
            pltpu.VMEM((steps, block, fj), bf16),
            pltpu.VMEM((cols - 1, rows, fi), bf16),
            pltpu.VMEM((cols - 1, rows, fi), bf16),
            pltpu.VMEM((SLOTS, fi, TILE), jnp.float32),
            dma((SLOTS,)),
            dma((cols - 1,)), dma((cols - 1,)),
            dma((steps, PIECES)), dma((steps, PIECES)),
            dma((chips, PIECES)), dma((chips, PIECES)),
            dma((cols, 2)), dma((cols, 2)),
            dma((steps, PIECES)), dma((steps, PIECES)),
            dma((cols - 1,)), dma((cols - 1,)),
        ],
        compiler_params=pltpu.CompilerParams(
            collective_id=0, has_side_effects=True, vmem_limit_bytes=67043328
        ),
    )(e1, e2, g)


def solution(mesh):
    return jax.shard_map(
        functools.partial(local, mesh.shape["row"], mesh.shape["col"]),
        mesh=mesh,
        in_specs=(P("col", "row"), P("row", "col"), P("row", "col")),
        out_specs=(P("col", "row"), P("row", "col")),
        check_vma=False,
    )
```

time: 443 us -> 145 us (0.33)
  waiting for transfers between devices: 375 us -> 0 us
  Pallas kernels: 0 us -> 140 us
  matrix products: 49.2 us -> 0 us
  between operations: 13.8 us -> 0.64 us
  other arithmetic: 4.77 us -> 0 us
    reduce_scatter x2 -> x0, waiting for transfers between devices: 264 us -> none  [the longest x1 245 us: local(): lax.psum_scatter(jnp.dot(whole_first, low_grad, preferred_element_type=jn...]
    pallas_call x0 -> x1, Pallas kernels: none -> 140 us  [local(): pl.pallas_call(functools.partial(kernel, a_side, b_side, cols, min(EARLY,...]
    all_gather x2 -> x0, waiting for transfers between devices: 110 us -> none  [the longest x1 105 us: local(): lax.all_gather(embed_second, 'row', axis=0, tiled=True)]
    dot_general x2 -> x0, matrix products: 49.2 us -> none  [the longest x1 27.3 us: local(): jnp.dot(whole_first, low_grad, preferred_element_type=jnp.float32)]
    convert_element_type x2 -> x0, other arithmetic: 4.77 us -> none  [the longest x1 2.41 us: local(): lax.psum_scatter(first_terms, 'col', scatter_dimension=0, tiled=True)]
  transfers between devices with their start and end apart: 4 -> 0, of which waited for: 4 -> 0; matrix products, arithmetic and copies ran while one was open for 12% -> 0% of each run, Pallas kernels for 0% -> 0%
where the time goes in v1:
time: 145 us
  Pallas kernels  140 us (97%)
  local copies, waits for them, and re-layouts  4.13 us (3%)
    pallas_call x1, Pallas kernels, local(): pl.pallas_call(functools.partial(kernel, a_side, b_side, cols, min(EARLY,...  140 us
    unnamed x2, local copies, waits for them, and re-layouts  4.13 us

profile of v1, /device:TPU:0, one launch (start us, length us, event | category | flops | bytes accessed | tf_op | source)
XLA Modules:
  0.0 144.6 jit_solution(13372599380868915319)
XLA Ops:
  0.6 139.8 %shard_map.50 = (bf16[384,1024]{1,0:T(8,128)(2,1)}, bf16[48,8192]{1,0:T(8,128)(2,1)}) custom-call(bf16[384,1024]{1,0:T(8,128)(2,1)} %e1_ref.1, bf16[48,8192]{1,0:T(8,128)(2,1)} %e2_ref.1, f32[1024,8192]{1,0:T(8,128)} %g_ref.1), custom_call_target="tpu_custom_call" | custom-call | tf_op jit(solution)/shard_map/pallas_call | solution.py:298
  140.5 2.1 %copy.7 = bf16[384,1024]{1,0:T(8,128)(2,1)} copy(bf16[384,1024]{1,0:T(8,128)(2,1)} %get-tuple-element.4) | data formatting | bytes 1572864
  142.5 2.1 %copy.8 = bf16[48,8192]{1,0:T(8,128)(2,1)} copy(bf16[48,8192]{1,0:T(8,128)(2,1)} %get-tuple-element.5) | data formatting | bytes 1572864

commit v2 on v1

v2 whole, which is shorter than its diff:
```python
import functools

import jax
import jax.numpy as jnp
from jax import lax
from jax.experimental import pallas as pl
from jax.experimental.pallas import tpu as pltpu
from jax.sharding import PartitionSpec as P

FIRST_SHARE = 0.4
TILE = 256
SLOTS = 3


def cuts(fj):
    unit = fj // 256
    short = round(unit * FIRST_SHARE)
    widths = [(True, short), (True, short), (False, unit - short), (False, unit - short)]
    out, at = [], 0
    for kind, w in widths:
        out.append((kind, at, w * 128))
        at += w * 128
    return out


def slots_of(side):
    return 1 if side == 2 else side + 1


def kernel(
    a_side, b_side, cols,
    e1_ref, e2_ref, g_ref, o1_ref, o2_ref,
    e1x, e2x, gb, p2, s2, rb_short, rb_long, acc, t1s, t1r, gt,
    g_sem, e1_send, e1_recv, ag_send, ag_recv, sib_send, sib_recv,
    d2d_send, d2d_recv, rs_send, rs_recv_short, rs_recv_long, t1_send, t1_recv,
):
    chips = a_side * b_side
    block, fj = e2_ref.shape
    rows, fi = e1_ref.shape
    share = chips // cols
    bf16, f32 = jnp.bfloat16, jnp.float32
    pieces = cuts(fj)
    order = [2, 0, 3, 1]
    sides = {"a": a_side, "b": b_side}

    me = lax.axis_index("row")
    my_col = lax.axis_index("col")
    chip, core = me // 2, me % 2
    other = 1 - core
    here = {"a": chip // b_side, "b": chip % b_side}
    sibling = chip * 2 + other

    def at_offset(da, db):
        return chip + da * b_side + db

    def neighbour(axis, sign):
        return (chip + sign * (b_side if axis == "a" else 1)) * 2 + core

    def inside(axis, d):
        where = here[axis] + d
        return jnp.logical_and(where >= 0, where < sides[axis])

    def both_inside(da, db):
        return jnp.logical_and(inside("a", da), inside("b", db))

    def offsets(distance):
        for da in range(a_side - 1, -a_side, -1):
            for db in range(b_side - 1, -b_side, -1):
                if abs(da) + abs(db) == distance:
                    yield da, db

    far = a_side + b_side - 2

    def piece(k):
        return pl.ds(pieces[k][1], pieces[k][2])

    def remote(src, dst, send, recv, **to):
        return pltpu.make_async_remote_copy(
            src_ref=src, dst_ref=dst, send_sem=send, recv_sem=recv,
            device_id=to, device_id_type=pl.DeviceIdType.MESH,
        )

    WAYS = (("a", 1), ("a", -1), ("b", 1), ("b", -1))

    barrier = pltpu.get_barrier_semaphore()
    for axis, sign in WAYS:
        @pl.when(inside(axis, sign))
        def _():
            pl.semaphore_signal(
                barrier, inc=1, device_id={"row": neighbour(axis, sign)}, device_id_type=pl.DeviceIdType.MESH
            )
    pl.semaphore_signal(barrier, inc=1, device_id={"row": sibling}, device_id_type=pl.DeviceIdType.MESH)
    for off in range(1, cols):
        pl.semaphore_signal(
            barrier, inc=1, device_id={"col": (my_col + off) % cols}, device_id_type=pl.DeviceIdType.MESH
        )
    peers = sum(inside(*way).astype(jnp.int32) for way in WAYS)
    pl.semaphore_wait(barrier, peers + cols)

    def block_copy(da, db, k, way):
        src_chip = at_offset(da, db)
        dst = e2x.at[src_chip, core, :, piece(k)]
        src = e2_ref.at[:, piece(k)] if (da, db) == (0, 0) else dst
        return remote(
            src, dst, ag_send.at[src_chip, k, way], ag_recv.at[src_chip, k], row=neighbour(*WAYS[way])
        )

    def sibling_copy(da, db, k):
        src_chip = at_offset(da, db)
        dst = e2x.at[src_chip, core, :, piece(k)]
        src = e2_ref.at[:, piece(k)] if (da, db) == (0, 0) else dst
        return remote(src, dst, sib_send.at[src_chip, k], sib_recv.at[src_chip, k], row=sibling)

    def onward(da, db, k):
        first, second = ("b", "a") if pieces[k][0] else ("a", "b")
        d = {"a": da, "b": db}
        for way, (axis, sign) in enumerate(WAYS):
            if axis == second:
                if d[second] * sign <= 0:
                    yield way
            elif d[second] == 0 and d[first] * sign <= 0:
                yield way

    def send_on(da, db, k):
        for way in onward(da, db, k):
            @pl.when(inside(*WAYS[way]))
            def _():
                block_copy(da, db, k, way).start()

    def gather_round(distance):
        for da, db in offsets(distance):
            @pl.when(both_inside(da, db))
            def _():
                for k in order:
                    block_copy(da, db, k, 0).wait_recv()
                    send_on(da, db, k)
                    sibling_copy(da, db, k).start()

    for k in order:
        send_on(0, 0, k)
    e1_copies = []
    for off in range(1, cols):
        to = (my_col + off) % cols
        e1_copies.append(remote(e1_ref, e1x.at[off - 1], e1_send.at[off - 1], e1_recv.at[off - 1], col=to))
        e1_copies[-1].start()

    def load(n):
        slot = n % SLOTS
        return pltpu.make_async_copy(
            g_ref.at[:, pl.ds(pl.multiple_of(n * TILE, TILE), TILE)], gt.at[slot], g_sem.at[slot]
        )

    tiles = fj // TILE
    for n in range(SLOTS):
        load(n).start()
    for k in order:
        sibling_copy(0, 0, k).start()

    def first_pass(n, carry):
        load(n).wait()
        at = pl.ds(pl.multiple_of(n * TILE, TILE), TILE)
        low = gt[n % SLOTS].astype(bf16)
        gb[:, at] = low

        @pl.when(n + SLOTS < tiles)
        def _():
            load(n + SLOTS).start()

        terms = jnp.dot(e1_ref[...], low, preferred_element_type=f32).astype(bf16)
        p2[pl.ds(my_col * share, share), :, :, at] = terms.reshape(share, 2, block, TILE)
        return carry

    def next_pass(off, wide):
        from_col = (my_col - off + cols) % cols

        def body(n, carry):
            at = pl.ds(pl.multiple_of(n * wide, wide), wide)
            terms = jnp.dot(e1x[off - 1], gb[:, at], preferred_element_type=f32).astype(bf16)
            p2[pl.ds(from_col * share, share), :, :, at] = terms.reshape(share, 2, block, wide)
            return carry

        return body

    def d2d_copy(off, h):
        from_chip = pl.ds((my_col - off + cols) % cols * share, share)
        at = pl.ds(h * (fj // 2), fj // 2)
        return remote(
            p2.at[from_chip, other, :, at], s2.at[from_chip, :, at],
            d2d_send.at[off, h], d2d_recv.at[off, h], row=sibling,
        )

    for h in range(2):
        lax.fori_loop(h * tiles // 2, (h + 1) * tiles // 2, first_pass, 0)
        d2d_copy(0, h).start()
    gather_round(1)
    e2x[chip, core] = e2_ref[...]
    wide = 512
    for off in range(1, cols):
        e1_copies[off - 1].wait_recv()
        for h in range(2):
            lax.fori_loop(h * fj // wide // 2, (h + 1) * fj // wide // 2, next_pass(off, wide), 0)
            d2d_copy(off, h).start()
    for off in range(cols):
        for h in range(2):
            d2d_copy(off, h).wait_recv()

    def sum_slot(k, axis, sign, to):
        short = pieces[k][0]
        first, second = ("a", "b") if short else ("b", "a")
        place = to["a"] if axis == "a" else to["b"]
        slot = 0 if sides[axis] == 2 else (place + 1 if sign > 0 else place)
        if axis == first:
            slot = to[second] * slots_of(sides[first]) + slot
        else:
            slot = sides[second] * slots_of(sides[first]) + slot
        start = pieces[k][1] if short else pieces[k][1] - pieces[2][1]
        buf = rb_short if short else rb_long
        sem = rs_recv_short if short else rs_recv_long
        return buf.at[slot, :, pl.ds(start, pieces[k][2])], sem.at[slot, k % 2]

    def place_of(da, db):
        return {"a": here["a"] + da, "b": here["b"] + db}

    def way_out(da, db, k):
        first, second = ("a", "b") if pieces[k][0] else ("b", "a")
        d = {"a": da, "b": db}
        axis = first if d[first] else second
        return axis, (1 if d[axis] > 0 else -1)

    def sum_copy(da, db, k):
        axis, sign = way_out(da, db, k)
        to_chip = at_offset(da, db)
        dst, sem = sum_slot(k, axis, sign, place_of(da, db))
        return remote(
            p2.at[to_chip, core, :, piece(k)], dst, rs_send.at[to_chip, k], sem, row=neighbour(axis, sign)
        )

    def arrivals(da, db, k):
        first, second = ("a", "b") if pieces[k][0] else ("b", "a")
        d = {"a": da, "b": db}
        out = []
        for sign in (1, -1):
            if d[first] * sign >= 0:
                out.append((first, sign))
        if d[first] == 0:
            for sign in (1, -1):
                if d[second] * sign >= 0:
                    out.append((second, sign))
        return out

    def sum_of(da, db, k):
        at = piece(k)
        to_chip = at_offset(da, db)
        kept = acc.at[:, pl.ds(0, pieces[k][2])]
        kept[...] = p2[to_chip, core, :, at].astype(f32) + s2[to_chip, :, at].astype(f32)
        for axis, sign in arrivals(da, db, k):
            @pl.when(inside(axis, -sign))
            def _():
                buf, sem = sum_slot(k, axis, sign, place_of(da, db))
                remote(buf, buf, rs_send.at[0, k], sem, row=sibling).wait_recv()
                kept[...] += buf[...].astype(f32)
        return kept[...].astype(bf16)

    def sum_round(distance):
        for da, db in offsets(distance):
            @pl.when(both_inside(da, db))
            def _():
                for k in order:
                    p2[at_offset(da, db), core, :, piece(k)] = sum_of(da, db, k)
                    sum_copy(da, db, k).start()

    left_to_sum = list(range(far, 0, -1))
    for distance in range(2, far + 1):
        sum_round(left_to_sum.pop(0))
        gather_round(distance)
    for da in range(1 - a_side, a_side):
        for db in range(1 - b_side, b_side):
            @pl.when(both_inside(da, db))
            def _():
                for k in range(4):
                    sibling_copy(da, db, k).wait_recv()

    def t1_copy(off):
        return remote(
            t1s.at[off - 1], t1r.at[off - 1], t1_send.at[off - 1], t1_recv.at[off - 1],
            col=(my_col + off) % cols,
        )

    def first_terms(of_col, n):
        left_side = e2x[pl.ds(of_col * share, share)].reshape(rows, fj)
        part = gb[pl.ds(pl.multiple_of(n * TILE, TILE), TILE), :]
        return lax.dot_general(left_side, part, (((1,), (1,)), ((), ())), preferred_element_type=f32)

    for off in range(1, cols):
        def send_body(n, carry, off=off):
            at = pl.ds(pl.multiple_of(n * TILE, TILE), TILE)
            t1s[off - 1, :, at] = first_terms((my_col + off) % cols, n).astype(bf16)
            return carry

        lax.fori_loop(0, fi // TILE, send_body, 0)
        t1_copy(off).start()
        if left_to_sum:
            sum_round(left_to_sum.pop(0))

    def keep(n):
        return gt.at[n // 2, pl.ds(pl.multiple_of(n % 2 * rows, rows), rows)]

    def own_body(n, carry):
        keep(n)[...] = first_terms(my_col, n)
        return carry

    lax.fori_loop(0, fi // TILE, own_body, 0)
    while left_to_sum:
        sum_round(left_to_sum.pop(0))

    for off in range(1, cols):
        t1_copy(off).wait_recv()

    def out_body(n, carry):
        at = pl.ds(pl.multiple_of(n * TILE, TILE), TILE)
        total = keep(n)[...]
        for off in range(1, cols):
            total += t1r[off - 1, :, at].astype(f32)
        o1_ref[:, at] = total.astype(bf16)
        return carry

    lax.fori_loop(0, fi // TILE, out_body, 0)

    for k in order:
        o2_ref[:, piece(k)] = sum_of(0, 0, k)

    for da in range(1 - a_side, a_side):
        for db in range(1 - b_side, b_side):
            @pl.when(both_inside(da, db))
            def _():
                for k in range(4):
                    for way in onward(da, db, k):
                        @pl.when(inside(*WAYS[way]))
                        def _():
                            block_copy(da, db, k, way).wait_send()
                    sibling_copy(da, db, k).wait_send()
                    if (da, db) != (0, 0):
                        sum_copy(da, db, k).wait_send()
    for off in range(cols):
        for h in range(2):
            d2d_copy(off, h).wait_send()
    for off in range(1, cols):
        e1_copies[off - 1].wait_send()
        t1_copy(off).wait_send()


def local(rows_size, cols, e1, e2, g):
    chips = rows_size // 2
    a_side = 4
    b_side = chips // a_side
    block, fj = e2.shape
    rows, fi = e1.shape
    bf16 = jnp.bfloat16
    vmem = pl.BlockSpec(memory_space=pltpu.VMEM)
    dma = pltpu.SemaphoreType.DMA
    pieces = cuts(fj)
    short, long = 2 * pieces[0][2], 2 * pieces[2][2]
    short_slots = b_side * slots_of(a_side) + slots_of(b_side)
    long_slots = a_side * slots_of(b_side) + slots_of(a_side)
    return pl.pallas_call(
        functools.partial(kernel, a_side, b_side, cols),
        out_shape=(jax.ShapeDtypeStruct(e1.shape, bf16), jax.ShapeDtypeStruct(e2.shape, bf16)),
        in_specs=[vmem, vmem, pl.BlockSpec(memory_space=pl.ANY)],
        out_specs=(vmem, vmem),
        scratch_shapes=[
            pltpu.VMEM((cols - 1, rows, fi), bf16),
            pltpu.VMEM((chips, 2, block, fj), bf16),
            pltpu.VMEM((fi, fj), bf16),
            pltpu.VMEM((chips, 2, block, fj), bf16),
            pltpu.VMEM((chips, block, fj), bf16),
            pltpu.VMEM((short_slots, block, short), bf16),
            pltpu.VMEM((long_slots, block, long), bf16),
            pltpu.VMEM((block, max(short, long) // 2), jnp.float32),
            pltpu.VMEM((cols - 1, rows, fi), bf16),
            pltpu.VMEM((cols - 1, rows, fi), bf16),
            pltpu.VMEM((SLOTS, fi, TILE), jnp.float32),
            dma((SLOTS,)),
            dma((cols - 1,)), dma((cols - 1,)),
            dma((chips, 4, 4)), dma((chips, 4)),
            dma((chips, 4)), dma((chips, 4)),
            dma((cols, 2)), dma((cols, 2)),
            dma((chips, 4)), dma((short_slots, 2)), dma((long_slots, 2)),
            dma((cols - 1,)), dma((cols - 1,)),
        ],
        compiler_params=pltpu.CompilerParams(
            collective_id=0, has_side_effects=True, vmem_limit_bytes=67043328
        ),
    )(e1, e2, g)


def solution(mesh):
    return jax.shard_map(
        functools.partial(local, mesh.shape["row"], mesh.shape["col"]),
        mesh=mesh,
        in_specs=(P("col", "row"), P("row", "col"), P("row", "col")),
        out_specs=(P("col", "row"), P("row", "col")),
        check_vma=False,
    )
```

time: 145 us -> 121 us (0.83)
  Pallas kernels: 140 us -> 116 us
    pallas_call x1, Pallas kernels: 140 us -> 116 us  [local(): pl.pallas_call(functools.partial(kernel, a_side, b_side, cols), out_shape...]
where the time goes in v2:
time: 121 us
  Pallas kernels  116 us (96%)
  local copies, waits for them, and re-layouts  4.13 us (3%)
    pallas_call x1, Pallas kernels, local(): pl.pallas_call(functools.partial(kernel, a_side, b_side, cols), out_shape...  116 us
    unnamed x2, local copies, waits for them, and re-layouts  4.13 us

profile of v2, /device:TPU:0, one launch (start us, length us, event | category | flops | bytes accessed | tf_op | source)
XLA Modules:
  0.0 121.0 jit_solution(4164108084619500900)
XLA Ops:
  0.6 116.2 %shard_map.50 = (bf16[384,1024]{1,0:T(8,128)(2,1)}, bf16[48,8192]{1,0:T(8,128)(2,1)}) custom-call(bf16[384,1024]{1,0:T(8,128)(2,1)} %e1_ref.1, bf16[48,8192]{1,0:T(8,128)(2,1)} %e2_ref.1, f32[1024,8192]{1,0:T(8,128)} %g_ref.1), custom_call_target="tpu_custom_call" | custom-call | tf_op jit(solution)/shard_map/pallas_call | solution.py:365
  116.8 2.1 %copy.7 = bf16[384,1024]{1,0:T(8,128)(2,1)} copy(bf16[384,1024]{1,0:T(8,128)(2,1)} %get-tuple-element.4) | data formatting | bytes 1572864
  118.9 2.1 %copy.8 = bf16[48,8192]{1,0:T(8,128)(2,1)} copy(bf16[48,8192]{1,0:T(8,128)(2,1)} %get-tuple-element.5) | data formatting | bytes 1572864
